TPU v7x, 32 devices: a whole 2x2x4 slice. The times are simulated.
32 devices in a mesh: gx: 8 (over z, y), gy: 4 (over x, core).
Axes of the slice: x: 2, y: 2, z: 4, core: 2. Of those that a mesh axis runs over, the one named last changes fastest.
Arguments:
- scalar: float32 [2, 512, 8, 4, 128], P(None, None, 'gx', 'gy'), may hold values from -6 to 6
- velocity: float32 [3, 2, 512, 8, 4, 128], P(None, None, None, 'gx', 'gy'), may hold values from -1 to 1
- diffusivity: float32 [2, 8, 4, 128], P(None, 'gx', 'gy'), may hold values from 0.005 to 0.05
- recv_owner: int32 [65536, 1], P(('gx', 'gy')), may hold values from 0 to 31; in each aligned block of 2048 rows (0 to 2047, 2048 to 4095, ...) at most 128 rows name the same one
- donor_elem: int32 [65536], P(('gx', 'gy')), may hold values from 0 to 127
- recv_point: int32 [65536], P(('gx', 'gy')), may hold values from 0 to 65535
- recv_coords: float32 [3, 65536], P(None, ('gx', 'gy')), may hold values from -1 to 1
Outputs:
- advanced: float32 [2, 512, 8, 4, 128], P(None, None, 'gx', 'gy')
Inputs may be any that keep to these rules, and one draw needn't show every extreme that they name: `recv_owner`: among the 2048 receivers of one device no owner is named more than 128 times, a bound that some block reaches.
All inputs are finite; a program needn't handle non-finite values.
Results may differ from a plain program's by a relative error of at most 0.0003.
Values sent between devices are 32-bit elements; how exact they have to be, the bound alone decides.
A program may use at most 128 MiB of HBM per device.

v0:
```python
import jax
import jax.numpy as jnp
from jax import lax
from jax.sharding import PartitionSpec as P

time_step = 0.01
penalty_rate = 50.0
metric = 2.0
volume_factor = 0.125
node_inner = [0.8717401485096066, 0.5917001814331423, 0.20929921790247888]


def passed_along(value, axis, steps):
    count = lax.axis_size(axis)
    leading, last = (max(0, -steps), min(count, count - steps))
    return lax.ppermute(value, axis, [(source, source + steps) for source in range(leading, last)])


def legendre_seven(point):
    before, current = (1.0, point)
    for order in range(1, 7):
        before, current = (
            current,
            ((2 * order + 1) * point * current - order * before) / (order + 1),
        )
    return current


def gll_tables():
    degree = 7
    gll_nodes = [
        -1.0,
        -node_inner[0],
        -node_inner[1],
        -node_inner[2],
        node_inner[2],
        node_inner[1],
        node_inner[0],
        1.0,
    ]
    end_values = [legendre_seven(v) for v in gll_nodes]
    weights = [2.0 / (degree * (degree + 1) * v * v) for v in end_values]
    derivative = [[0.0] * 8 for _ in range(8)]
    for a in range(8):
        for b in range(8):
            if a != b:
                derivative[a][b] = end_values[a] / (end_values[b] * (gll_nodes[a] - gll_nodes[b]))
    derivative[0][0] = -degree * (degree + 1) / 4.0
    derivative[7][7] = degree * (degree + 1) / 4.0
    weight_row = jnp.asarray(weights, jnp.float32)
    cube_weights = weight_row[:, None, None] * weight_row[None, :, None] * weight_row[None, None, :]
    return (gll_nodes, cube_weights, derivative)


def lagrange_rows(position, gll_nodes):
    columns = []
    for j in range(8):
        factor = jnp.ones_like(position)
        for m in range(8):
            if m != j:
                factor = factor * ((position - gll_nodes[m]) / (gll_nodes[j] - gll_nodes[m]))
        columns.append(factor)
    return jnp.stack(columns, axis=-1)


def element_rate(values, velocity, diffusivity, derivative, cube_weights):
    highest = lax.Precision.HIGHEST
    grad_x = metric * jnp.einsum("ai,ijkxyz->ajkxyz", derivative, values, precision=highest)
    grad_y = metric * jnp.einsum("bj,ijkxyz->ibkxyz", derivative, values, precision=highest)
    grad_z = metric * jnp.einsum("ck,ijkxyz->ijcxyz", derivative, values, precision=highest)
    mass_local = volume_factor * cube_weights[:, :, :, None, None, None]
    advect = velocity[0] * grad_x + velocity[1] * grad_y + velocity[2] * grad_z
    scaled = metric * mass_local * diffusivity[None, None, None]
    diffuse = jnp.einsum("ai,ajkxyz->ijkxyz", derivative, scaled * grad_x, precision=highest)
    diffuse = diffuse + jnp.einsum(
        "bj,ibkxyz->ijkxyz", derivative, scaled * grad_y, precision=highest
    )
    diffuse = diffuse + jnp.einsum(
        "ck,ijcxyz->ijkxyz", derivative, scaled * grad_z, precision=highest
    )
    return -(mass_local * advect) - diffuse


def face_sum(values, pdim, edim, next_slab, prev_slab):
    left = lax.index_in_dim(values, 0, pdim, keepdims=True)
    right = lax.index_in_dim(values, 7, pdim, keepdims=True)
    count = values.shape[edim]
    after = jnp.concatenate([lax.slice_in_dim(left, 1, count, axis=edim), next_slab], axis=edim)
    before = jnp.concatenate(
        [prev_slab, lax.slice_in_dim(right, 0, count - 1, axis=edim)], axis=edim
    )
    middle = lax.slice_in_dim(values, 1, 7, axis=pdim)
    return jnp.concatenate([left + before, middle, right + after], axis=pdim)


def edge_slabs(values, pdim, edim):
    left = lax.index_in_dim(values, 0, pdim, keepdims=True)
    right = lax.index_in_dim(values, 7, pdim, keepdims=True)
    count = values.shape[edim]
    return (
        lax.index_in_dim(left, 0, edim, keepdims=True),
        lax.index_in_dim(right, count - 1, edim, keepdims=True),
    )


def assemble(values):
    left_first, right_last = edge_slabs(values, 1, 4)
    next_slab = passed_along(left_first, "gx", -1)
    prev_slab = passed_along(right_last, "gx", 1)
    values = face_sum(values, 1, 4, next_slab, prev_slab)
    left_first, right_last = edge_slabs(values, 2, 5)
    next_slab = passed_along(left_first, "gy", -1)
    prev_slab = passed_along(right_last, "gy", 1)
    values = face_sum(values, 2, 5, next_slab, prev_slab)
    zeros_slab = jnp.zeros_like(edge_slabs(values, 3, 6)[0])
    return face_sum(values, 3, 6, zeros_slab, zeros_slab)


def body(scalar, velocity, diffusivity, recv_owner, donor_elem, recv_point, recv_coords):
    gll_nodes, cube_np, derivative_np = gll_tables()
    derivative = jnp.asarray(derivative_np, jnp.float32)
    cube_weights = jnp.asarray(cube_np, jnp.float32)
    cube_flat = cube_weights.reshape(512)
    count_x, count_y, count_z = (scalar.shape[2], scalar.shape[3], scalar.shape[4])
    elems = count_x * count_y * count_z
    shape_full = (2, 8, 8, 8, count_x, count_y, count_z)
    flow = velocity.reshape((3,) + shape_full)
    mass_total = assemble(
        jnp.broadcast_to(volume_factor * cube_weights[None, :, :, :, None, None, None], shape_full)
    )
    width_x = lax.axis_size("gx")
    width_y = lax.axis_size("gy")
    devices = width_x * width_y
    rows = recv_owner.shape[0]
    capacity = max(2, 2 * rows // devices)
    slots_all = devices * capacity
    owners = recv_owner[:, 0]
    one_hot = (owners[:, None] == jnp.arange(devices, dtype=jnp.int32)[None, :]).astype(jnp.int32)
    slots = jnp.sum(jnp.cumsum(one_hot, axis=0) * one_hot, axis=1) - 1
    target = owners * capacity + slots
    own_mesh = (jnp.arange(rows, dtype=jnp.int32) >= rows // 2).astype(jnp.int32)
    donor_ids = (1 - own_mesh) * elems + donor_elem
    queries = jnp.concatenate([recv_coords, donor_ids.astype(jnp.float32)[None]], axis=0)
    payload = jnp.zeros((4, slots_all), jnp.float32).at[:, target].set(queries)
    point_q = recv_point // elems
    flat_index = own_mesh * (512 * elems) + recv_point
    point_mass = volume_factor * cube_flat[point_q]
    received = lax.all_to_all(
        payload.reshape(4, devices, capacity), ("gx", "gy"), split_axis=1, concat_axis=1, tiled=True
    )
    received = received.reshape(4, slots_all)

    def send_answers(answers):
        moved = lax.all_to_all(
            answers.reshape(devices, capacity),
            ("gx", "gy"),
            split_axis=0,
            concat_axis=0,
            tiled=True,
        )
        return moved.reshape(slots_all)

    block_count = 1
    row_ids = received[3].astype(jnp.int32)
    kept = (
        row_ids,
        lagrange_rows(received[0], gll_nodes),
        lagrange_rows(received[1], gll_nodes),
        lagrange_rows(received[2], gll_nodes),
    )
    kept = tuple(
        (piece.reshape((block_count, slots_all // block_count) + piece.shape[1:]) for piece in kept)
    )

    def interpolate(values):
        element_rows = jnp.transpose(values.reshape(2, 512, elems), (0, 2, 1)).reshape(
            2 * elems, 512
        )

        def one_block(pieces):
            ids, wx, wy, wz = pieces
            element_values = element_rows[ids].reshape(-1, 8, 8, 8)
            return jnp.einsum(
                "nijk,ni,nj,nk->n", element_values, wx, wy, wz, precision=lax.Precision.HIGHEST
            )

        return lax.map(one_block, kept).reshape(slots_all)

    def rate(values):
        local = jnp.stack(
            [
                element_rate(values[m], flow[:, m], diffusivity[m], derivative, cube_weights)
                for m in range(2)
            ]
        )
        answers = interpolate(values)
        replies = send_answers(answers)
        donor_values = replies[target]
        current = values.reshape(-1)[flat_index]
        added = penalty_rate * point_mass * (donor_values - current)
        local = local.reshape(-1).at[flat_index].add(added).reshape(shape_full)
        return assemble(local) / mass_total

    start = scalar.reshape(shape_full)
    first = start + time_step * rate(start)
    second = 0.75 * start + 0.25 * (first + time_step * rate(first))
    third = start / 3.0 + 2.0 / 3.0 * (second + time_step * rate(second))
    return third.reshape(2, 512, count_x, count_y, count_z)


def solution(mesh):
    return jax.shard_map(
        body,
        mesh=mesh,
        in_specs=(
            P(None, None, "gx", "gy", None),
            P(None, None, None, "gx", "gy", None),
            P(None, "gx", "gy", None),
            P(("gx", "gy"), None),
            P(("gx", "gy")),
            P(("gx", "gy")),
            P(None, ("gx", "gy")),
        ),
        out_specs=P(None, None, "gx", "gy", None),
        check_vma=False,
    )
```

profile of v0, /device:TPU:9, one launch (start us, length us, event | category | flops | bytes accessed | tf_op | source)
XLA Modules:
  0.0 412.8 jit_solution(2832457730301252134)
XLA Ops:
  1.7 3.0 collective-permute-start.5
  4.9 2.2 collective-permute-start.4
  7.8 9.1 %reduce-window.6 = s32[32,16,128]{2,1,0:T(8,128)S(1)} reduce-window(s32[32,16,128]{2,1,0:T(8,128)S(1)} %fusion.137, s32[]{:T(128)} %constant.325.clone.1), window={size=1x1x128 pad=0_0x0_0x127_0}, to_apply=%region_0.0 | reduce-window | flops 8323072 | bytes 524292 | tf_op jit(solution)/shard_map/reduce-window
  22.0 6.5 %scatter_custom_fusion = f32[4,4096]{0,1:T(8,128)S(1)} fusion(s32[2048]{0:T(1024)S(1)} %bitcast.656, f32[2048,4]{1,0:T(8,128)} %copy.900, f32[]{:T(128)} %constant.333.clone.1), kind=kCustom, calls=%fused_computation.52 | custom fusion | bytes 66048 | tf_op jit(solution)/shard_map/scatter | solution.py:144
  29.7 7.4 %all-to-all-start = ((f32[4,32,128]{2,0,1:T(4,128)}), f32[4,32,128]{2,0,1:T(4,128)S(1)}, u32[]{:S(2)}, u32[]{:S(2)}) async-start(f32[4,32,128]{2,0,1:T(4,128)} %copy.901), calls=%async_computation | async-start | bytes 131072 | tf_op jit(solution)/shard_map/all_to_all | solution.py:148
  41.9 2.3 slice_bitcast_fusion.12
  49.6 11.8 %gather_fusion.3 = f32[2048]{0:T(1024)S(1)} fusion(f32[131072]{0:T(1024)S(1)} %bitcast.576, s32[2048]{0:T(1024)S(1)} %get-tuple-element.170), kind=kCustom, calls=%fused_computation.3 | custom fusion | bytes 24576 | tf_op jit(solution)/shard_map/gather | solution.py:199
  61.4 13.2 %gather_fusion = f32[2048]{0:T(1024)S(1)} fusion(f32[512]{0:T(512)S(1)} %mul.2271, s32[2048]{0:T(1024)S(1)} %get-tuple-element.169), kind=kCustom, calls=%fused_computation | custom fusion | bytes 24576 | tf_op jit(solution)/shard_map/gather | solution.py:147
  75.1 3.4 collective-permute-start.6
  78.7 16.8 %gather_fusion.1 = f32[4096,512]{1,0:T(8,128)} fusion(f32[256,512]{1,0:T(8,128)S(1)} %bitcast.568, s32[4096]{0:T(1024)S(1)} %broadcast_clamp_fusion), kind=kCustom, calls=%fused_computation.1 | custom fusion | bytes 16793600 | tf_op jit(solution)/shard_map/while/body/eval_jaxpr/gather | solution.py:182
  95.5 8.9 %copy.905 = f32[4096,512]{0,1:T(8,128)} copy(f32[4096,512]{1,0:T(8,128)} %gather_fusion.1) | data formatting | bytes 16777216 | tf_op jit(solution)/shard_map/while/body/eval_jaxpr/gather | solution.py:182
  105.7 4.1 %multiply_reduce_fusion.2 = f32[4096,8]{0,1:T(8,128)S(1)} fusion(f32[4096,8,8,8]{0,3,2,1:T(8,128)} %bitcast.593, f32[4096,8,8]{0,2,1:T(8,128)S(1)} %copy.1089), kind=kLoop, calls=%fused_computation.16 | loop fusion | flops 4161536 | bytes 9568256 | tf_op jit(solution)/shard_map/while/body/eval_jaxpr/nijk,ni,nj,nk->n/dot_general | solution.py:183
  110.7 4.7 %all-to-all-start.1 = ((f32[32,1,128]{2,1,0:T(1,128)}), f32[32,1,128]{2,1,0:T(1,128)S(1)}, u32[]{:S(2)}, u32[]{:S(2)}) async-start(f32[32,1,128]{2,1,0:T(1,128)} %bitcast.107), calls=%async_computation.1 | async-start | bytes 32768 | tf_op jit(solution)/shard_map/all_to_all | solution.py:154
  116.2 2.3 collective-permute-start.7
  118.5 2.3 all-to-all-done.1
  120.9 11.8 %gather_fusion.2 = f32[2048]{0:T(1024)S(1)} fusion(f32[4096]{0:T(1024)S(1)} %bitcast.573, s32[2048]{0:T(1024)S(1)} %broadcast_clamp_fusion.2), kind=kCustom, calls=%fused_computation.2 | custom fusion | bytes 24576 | tf_op jit(solution)/shard_map/gather | solution.py:198
  132.7 11.7 %scatter_fusion = f32[131072]{0:T(1024)S(1)} fusion(f32[131072]{0:T(1024)S(1)} %bitcast.584, s32[2048]{0:T(1024)S(1)} %get-tuple-element.171, f32[2048]{0:T(1024)S(1)} %subtract_multiply_fusion.2), kind=kCustom, calls=%fused_computation.11 | custom fusion | flops 2048 | bytes 32768 | tf_op jit(solution)/shard_map/scatter-add | solution.py:201
  144.6 3.3 collective-permute-start.1
  150.5 3.5 collective-permute-done
  154.1 4.4 %collective-permute-start.2 = (f32[2,8,1,8,1,1,128]{6,1,3,2,5,4,0:T(8,128)S(1)}, f32[2,8,1,8,1,1,128]{6,1,3,2,5,4,0:T(8,128)S(1)}, u32[]{:S(2)}, u32[]{:S(2)}) collective-permute-start(f32[2,8,1,8,1,1,128]{6,1,3,2,5,4,0:T(8,128)S(1)} %pad_maximum_fusion.10), channel_id=1, source_target_pairs={{0,1},{1,2},{2,3},{4,5},{5,6},{6,7},{8,9},{9,10},{10,11},{12,13},{... | collective-permute-start | bytes 196616 | tf_op jit(solution)/shard_map/ppermute | solution.py:16
  161.9 4.1 %collective-permute-done.3 = f32[2,8,1,8,1,1,128]{6,1,3,2,5,4,0:T(8,128)S(1)} collective-permute-done((f32[2,8,1,8,1,1,128]{6,1,3,2,5,4,0:T(8,128)S(1)}, f32[2,8,1,8,1,1,128]{6,1,3,2,5,4,0:T(8,128)S(1)}, u32[]{:S(2)}, u32[]{:S(2)}) %collective-permute-start.3) | collective-permute-done | bytes 65568 | tf_op jit(solution)/shard_map/ppermute | solution.py:16
  180.3 18.0 %gather_fusion.4 = f32[4096,512]{1,0:T(8,128)} fusion(f32[256,512]{1,0:T(8,128)S(1)} %bitcast.570, s32[4096]{0:T(1024)} %copy-done.42), kind=kCustom, calls=%fused_computation.4 | custom fusion | bytes 16793600 | tf_op jit(solution)/shard_map/while/body/eval_jaxpr/gather | solution.py:182
  198.3 8.9 %copy.951 = f32[4096,512]{0,1:T(8,128)} copy(f32[4096,512]{1,0:T(8,128)} %gather_fusion.4) | data formatting | bytes 16777216 | tf_op jit(solution)/shard_map/while/body/eval_jaxpr/gather | solution.py:182
  207.3 4.2 %multiply_reduce_fusion.1 = f32[4096,8]{0,1:T(8,128)S(1)} fusion(f32[4096,8,8,8]{0,3,2,1:T(8,128)} %bitcast.595, f32[4096,8,8]{0,2,1:T(8,128)S(1)} %copy.1089), kind=kLoop, calls=%fused_computation.15 | loop fusion | flops 4161536 | bytes 9568256 | tf_op jit(solution)/shard_map/while/body/eval_jaxpr/nijk,ni,nj,nk->n/dot_general | solution.py:183
  212.1 2.2 all-to-all-start.2
  214.4 2.2 fusion.12
  216.7 2.6 fusion.16
  219.5 20.6 %gather_fusion.6 = f32[2048]{0:T(1024)} fusion(f32[131072]{0:T(1024)S(1)} %add.1140, s32[2048]{0:T(1024)} %copy-done.48), kind=kCustom, calls=%fused_computation.6 | custom fusion | bytes 24576 | tf_op jit(solution)/shard_map/gather | solution.py:199
  240.1 20.6 %gather_fusion.5 = f32[2048]{0:T(1024)} fusion(f32[4096]{0:T(1024)S(1)} %bitcast.572, s32[2048]{0:T(1024)} %copy-done.47), kind=kCustom, calls=%fused_computation.5 | custom fusion | bytes 24576 | tf_op jit(solution)/shard_map/gather | solution.py:198
  261.5 11.9 %scatter_fusion.1 = f32[131072]{0:T(1024)S(1)} fusion(f32[131072]{0:T(1024)S(1)} %bitcast.590, s32[2048]{0:T(1024)} %copy-done.43, f32[2048]{0:T(1024)S(1)} %subtract_multiply_fusion.1), kind=kCustom, calls=%fused_computation.12 | custom fusion | flops 2048 | bytes 32768 | tf_op jit(solution)/shard_map/scatter-add | solution.py:201
  273.4 2.7 collective-permute-start.9
  276.1 2.5 collective-permute-start.8
  279.1 3.0 collective-permute-done.8
  282.1 4.8 %collective-permute-start.10 = (f32[2,8,1,8,1,1,128]{6,1,3,2,5,4,0:T(8,128)S(1)}, f32[2,8,1,8,1,1,128]{6,1,3,2,5,4,0:T(8,128)S(1)}, u32[]{:S(2)}, u32[]{:S(2)}) collective-permute-start(f32[2,8,1,8,1,1,128]{6,1,3,2,5,4,0:T(8,128)S(1)} %pad_maximum_fusion.6), channel_id=1, source_target_pairs={{0,1},{1,2},{2,3},{4,5},{5,6},{6,7},{8,9},{9,10},{10,11},{12,13},{... | collective-permute-start | bytes 196616 | tf_op jit(solution)/shard_map/ppermute | solution.py:16
  290.4 4.1 collective-permute-done.11
  309.9 18.0 %gather_fusion.7 = f32[4096,512]{1,0:T(8,128)} fusion(f32[256,512]{1,0:T(8,128)S(1)} %bitcast.569, s32[4096]{0:T(1024)} %copy-done.42), kind=kCustom, calls=%fused_computation.7 | custom fusion | bytes 16793600 | tf_op jit(solution)/shard_map/while/body/eval_jaxpr/gather | solution.py:182
  327.9 8.9 %copy.993 = f32[4096,512]{0,1:T(8,128)} copy(f32[4096,512]{1,0:T(8,128)} %gather_fusion.7) | data formatting | bytes 16777216 | tf_op jit(solution)/shard_map/while/body/eval_jaxpr/gather | solution.py:182
  336.8 4.2 %multiply_reduce_fusion = f32[4096,8]{0,1:T(8,128)S(1)} fusion(f32[4096,8,8,8]{0,3,2,1:T(8,128)} %bitcast.594, f32[4096,8,8]{0,2,1:T(8,128)S(1)} %copy.1089), kind=kLoop, calls=%fused_computation.14 | loop fusion | flops 4161536 | bytes 9568256 | tf_op jit(solution)/shard_map/while/body/eval_jaxpr/nijk,ni,nj,nk->n/dot_general | solution.py:183
  341.7 3.7 all-to-all-start.3
  346.5 3.1 fusion.24
  349.6 2.7 fusion.20
  352.5 12.0 %gather_fusion.9 = f32[2048]{0:T(1024)S(1)} fusion(f32[131072]{0:T(1024)S(1)} %multiply_add_fusion, s32[2048]{0:T(1024)} %copy-done.48), kind=kCustom, calls=%fused_computation.9 | custom fusion | bytes 24576 | tf_op jit(solution)/shard_map/gather | solution.py:199
  364.6 11.9 %gather_fusion.8 = f32[2048]{0:T(1024)S(1)} fusion(f32[4096]{0:T(1024)S(1)} %bitcast.571, s32[2048]{0:T(1024)} %copy-done.47), kind=kCustom, calls=%fused_computation.8 | custom fusion | bytes 24576 | tf_op jit(solution)/shard_map/gather | solution.py:198
  376.5 12.0 %scatter_fusion.2 = f32[131072]{0:T(1024)S(1)} fusion(f32[131072]{0:T(1024)S(1)} %bitcast.587, s32[2048]{0:T(1024)S(1)} %copy-done.44, f32[2048]{0:T(1024)S(1)} %subtract_multiply_fusion), kind=kCustom, calls=%fused_computation.13 | custom fusion | flops 2048 | bytes 32768 | tf_op jit(solution)/shard_map/scatter-add | solution.py:201
  388.5 3.2 collective-permute-start.13
  394.3 3.3 collective-permute-done.12
  397.8 4.8 %collective-permute-start.14 = (f32[2,8,1,8,1,1,128]{6,1,3,2,5,4,0:T(8,128)S(1)}, f32[2,8,1,8,1,1,128]{6,1,3,2,5,4,0:T(8,128)S(1)}, u32[]{:S(2)}, u32[]{:S(2)}) collective-permute-start(f32[2,8,1,8,1,1,128]{6,1,3,2,5,4,0:T(8,128)S(1)} %pad_maximum_fusion.4), channel_id=1, source_target_pairs={{0,1},{1,2},{2,3},{4,5},{5,6},{6,7},{8,9},{9,10},{10,11},{12,13},{... | collective-permute-start | bytes 196616 | tf_op jit(solution)/shard_map/ppermute | solution.py:16
  405.9 4.3 %collective-permute-done.15 = f32[2,8,1,8,1,1,128]{6,1,3,2,5,4,0:T(8,128)S(1)} collective-permute-done((f32[2,8,1,8,1,1,128]{6,1,3,2,5,4,0:T(8,128)S(1)}, f32[2,8,1,8,1,1,128]{6,1,3,2,5,4,0:T(8,128)S(1)}, u32[]{:S(2)}, u32[]{:S(2)}) %collective-permute-start.15) | collective-permute-done | bytes 65568 | tf_op jit(solution)/shard_map/ppermute | solution.py:16
  (294 shorter events, 73.3 us)
Async XLA Ops:
  0.0 37.9 %copy-start.3 = (f32[8,8,1,1]{1,0,3,2:T(8,128)S(1)}, f32[8,8,1,1]{1,0,3,2:T(8,128)}, u32[]{:S(2)}) copy-start(f32[8,8,1,1]{1,0,3,2:T(8,128)} %constant.406) | copy-start | bytes 772
  0.0 37.9 %copy-start = (f32[2,512,1,1,128]{4,3,2,1,0:T(1,128)S(1)}, f32[2,512,1,1,128]{4,3,2,1,0:T(1,128)}, u32[]{:S(2)}) copy-start(f32[2,512,1,1,128]{4,3,2,1,0:T(1,128)} %param.9) | copy-start | bytes 1572868
  0.0 40.0 %copy-start.59 = (f32[2,1,1,128]{3,2,1,0:T(1,128)S(1)}, f32[2,1,1,128]{3,2,1,0:T(1,128)}, u32[]{:S(2)}) copy-start(f32[2,1,1,128]{3,2,1,0:T(1,128)} %param.11) | copy-start | bytes 3076
  1.7 72.9 %collective-permute-start.5 = (f32[2,1,8,8,1,1,128]{6,1,3,2,5,4,0:T(1,128)S(1)}, f32[2,1,8,8,1,1,128]{6,1,3,2,5,4,0:T(1,128)S(1)}, u32[]{:S(2)}, u32[]{:S(2)}) collective-permute-start(f32[2,1,8,8,1,1,128]{6,1,3,2,5,4,0:T(1,128)S(1)} %broadcast_in_dim.30), channel_id=1, source_target_pairs={{4,0},{8,4},{12,8},{16,12},{20,16},{24,20},{28,24},{5,1},{9,5},{13... | collective-permute-start | bytes 196616 | tf_op jit(solution)/shard_map/ppermute | solution.py:16
  4.9 69.9 %collective-permute-start.4 = (f32[2,1,8,8,1,1,128]{6,1,3,2,5,4,0:T(1,128)S(1)}, f32[2,1,8,8,1,1,128]{6,1,3,2,5,4,0:T(1,128)S(1)}, u32[]{:S(2)}, u32[]{:S(2)}) collective-permute-start(f32[2,1,8,8,1,1,128]{6,1,3,2,5,4,0:T(1,128)S(1)} %broadcast_in_dim.32), channel_id=1, source_target_pairs={{0,4},{4,8},{8,12},{12,16},{16,20},{20,24},{24,28},{1,5},{5,9},{9,... | collective-permute-start | bytes 196616 | tf_op jit(solution)/shard_map/ppermute | solution.py:16
  17.5 26.8 %copy-start.56 = (f32[8,8,1,1]{1,0,2,3:T(8,128)S(1)}, f32[8,8,1,1]{1,0,2,3:T(8,128)}, u32[]{:S(2)}) copy-start(f32[8,8,1,1]{1,0,2,3:T(8,128)} %constant.407) | copy-start | bytes 772
  29.7 48.8 %all-to-all-start = ((f32[4,32,128]{2,0,1:T(4,128)}), f32[4,32,128]{2,0,1:T(4,128)S(1)}, u32[]{:S(2)}, u32[]{:S(2)}) async-start(f32[4,32,128]{2,0,1:T(4,128)} %copy.901), calls=%async_computation | async-start | bytes 131072 | tf_op jit(solution)/shard_map/all_to_all | solution.py:148
  40.0 80.9 %copy-start.47 = (s32[2048]{0:T(1024)}, s32[2048]{0:T(1024)S(1)}, u32[]{:S(2)}) copy-start(s32[2048]{0:T(1024)S(1)} %broadcast_clamp_fusion.2) | copy-start | bytes 24580
  47.0 85.7 %copy-start.43 = (s32[2048]{0:T(1024)}, s32[2048]{0:T(1024)S(1)}, u32[]{:S(2)}) copy-start(s32[2048]{0:T(1024)S(1)} %get-tuple-element.171) | copy-start | bytes 24580
  74.6 58.0 %copy-start.45 = (f32[2048]{0:T(1024)}, f32[2048]{0:T(1024)S(1)}, u32[]{:S(2)}) copy-start(f32[2048]{0:T(1024)S(1)} %gather_fusion) | copy-start | bytes 24580
  75.1 40.3 %collective-permute-start.6 = (f32[2,8,1,8,1,1,128]{6,1,3,2,5,4,0:T(8,128)S(1)}, f32[2,8,1,8,1,1,128]{6,1,3,2,5,4,0:T(8,128)}, u32[]{:S(2)}, u32[]{:S(2)}) collective-permute-start(f32[2,8,1,8,1,1,128]{6,1,3,2,5,4,0:T(8,128)S(1)} %pad_maximum_fusion.8), channel_id=1, source_target_pairs={{0,1},{1,2},{2,3},{4,5},{5,6},{6,7},{8,9},{9,10},{10,11},{12,13},{... | collective-permute-start | bytes 196616 | tf_op jit(solution)/shard_map/ppermute | solution.py:16
  110.7 10.2 %all-to-all-start.1 = ((f32[32,1,128]{2,1,0:T(1,128)}), f32[32,1,128]{2,1,0:T(1,128)S(1)}, u32[]{:S(2)}, u32[]{:S(2)}) async-start(f32[32,1,128]{2,1,0:T(1,128)} %bitcast.107), calls=%async_computation.1 | async-start | bytes 32768 | tf_op jit(solution)/shard_map/all_to_all | solution.py:154
  116.2 34.0 %collective-permute-start.7 = (f32[2,8,1,8,1,1,128]{6,1,3,2,5,4,0:T(8,128)S(1)}, f32[2,8,1,8,1,1,128]{6,1,3,2,5,4,0:T(8,128)S(1)}, u32[]{:S(2)}, u32[]{:S(2)}) collective-permute-start(f32[2,8,1,8,1,1,128]{6,1,3,2,5,4,0:T(8,128)S(1)} %get-tuple-element.61), channel_id=1, source_target_pairs={{1,0},{2,1},{3,2},{5,4},{6,5},{7,6},{9,8},{10,9},{11,10},{13,12},{... | collective-permute-start | bytes 196616 | tf_op jit(solution)/shard_map/ppermute | solution.py:16
  144.4 22.4 %copy-start.4 = (f32[8,8,1,1]{1,0,3,2:T(8,128)S(1)}, f32[8,8,1,1]{1,0,3,2:T(8,128)}, u32[]{:S(2)}) copy-start(f32[8,8,1,1]{1,0,3,2:T(8,128)} %constant.406) | copy-start | bytes 772
  144.4 24.6 %copy-start.21 = (f32[8,8,8]{0,2,1:T(8,128)S(1)}, f32[8,8,8]{0,2,1:T(8,128)}, u32[]{:S(2)}) copy-start(f32[8,8,8]{0,2,1:T(8,128)} %copy-done.20) | copy-start | bytes 6148
  144.5 24.6 %copy-start.50 = (f32[128]{0:T(128)S(1)}, f32[128]{0:T(128)}, u32[]{:S(2)}) copy-start(f32[128]{0:T(128)} %copy-done.49) | copy-start | bytes 1540
  144.5 24.6 %copy-start.53 = (f32[128]{0:T(128)S(1)}, f32[128]{0:T(128)}, u32[]{:S(2)}) copy-start(f32[128]{0:T(128)} %copy-done.52) | copy-start | bytes 1540
  144.5 26.0 %copy-start.12 = (f32[1,1,8,8,8,1,1,128]{7,4,3,2,1,0,6,5:T(8,128)S(1)}, f32[1,1,8,8,8,1,1,128]{7,4,3,2,1,0,6,5:T(8,128)}, u32[]{:S(2)}) copy-start(f32[1,1,8,8,8,1,1,128]{7,4,3,2,1,0,6,5:T(8,128)} %copy-done.11) | copy-start | bytes 786436
  144.5 26.0 %copy-start.27 = (f32[8,8,8,1,1,128]{5,0,2,1,4,3:T(8,128)S(1)}, f32[8,8,8,1,1,128]{5,0,2,1,4,3:T(8,128)}, u32[]{:S(2)}) copy-start(f32[8,8,8,1,1,128]{5,0,2,1,4,3:T(8,128)} %copy-done.26) | copy-start | bytes 786436
  144.6 5.8 %collective-permute-start.1 = (f32[2,1,8,8,1,1,128]{6,1,3,2,5,4,0:T(1,128)S(1)}, f32[2,1,8,8,1,1,128]{6,1,3,2,5,4,0:T(1,128)S(1)}, u32[]{:S(2)}, u32[]{:S(2)}) collective-permute-start(f32[2,1,8,8,1,1,128]{6,1,3,2,5,4,0:T(1,128)S(1)} %bitcast.610), channel_id=1, source_target_pairs={{4,0},{8,4},{12,8},{16,12},{20,16},{24,20},{28,24},{5,1},{9,5},{13... | collective-permute-start | bytes 196616 | tf_op jit(solution)/shard_map/ppermute | solution.py:16
  148.1 5.9 %collective-permute-start = (f32[2,1,8,8,1,1,128]{6,1,3,2,5,4,0:T(1,128)S(1)}, f32[2,1,8,8,1,1,128]{6,1,3,2,5,4,0:T(1,128)S(1)}, u32[]{:S(2)}, u32[]{:S(2)}) collective-permute-start(f32[2,1,8,8,1,1,128]{6,1,3,2,5,4,0:T(1,128)S(1)} %bitcast.612), channel_id=1, source_target_pairs={{0,4},{4,8},{8,12},{12,16},{16,20},{20,24},{24,28},{1,5},{5,9},{9,... | collective-permute-start | bytes 196616 | tf_op jit(solution)/shard_map/ppermute | solution.py:16
  154.1 20.6 %copy-start.41 = (f32[8,8,8,128]{3,0,2,1:T(8,128)S(1)}, f32[8,8,8,128]{3,0,2,1:T(8,128)}, u32[]{:S(2)}) copy-start(f32[8,8,8,128]{3,0,2,1:T(8,128)} %get-tuple-element.137) | copy-start | bytes 786436
  154.1 20.6 %copy-start.57 = (f32[8,8,1,1]{1,0,2,3:T(8,128)S(1)}, f32[8,8,1,1]{1,0,2,3:T(8,128)}, u32[]{:S(2)}) copy-start(f32[8,8,1,1]{1,0,2,3:T(8,128)} %constant.407) | copy-start | bytes 772
  154.1 5.7 %collective-permute-start.2 = (f32[2,8,1,8,1,1,128]{6,1,3,2,5,4,0:T(8,128)S(1)}, f32[2,8,1,8,1,1,128]{6,1,3,2,5,4,0:T(8,128)S(1)}, u32[]{:S(2)}, u32[]{:S(2)}) collective-permute-start(f32[2,8,1,8,1,1,128]{6,1,3,2,5,4,0:T(8,128)S(1)} %pad_maximum_fusion.10), channel_id=1, source_target_pairs={{0,1},{1,2},{2,3},{4,5},{5,6},{6,7},{8,9},{9,10},{10,11},{12,13},{... | collective-permute-start | bytes 196616 | tf_op jit(solution)/shard_map/ppermute | solution.py:16
  158.6 17.2 %copy-start.9 = (f32[1,1,8,8,8,1,1,128]{7,4,3,2,1,0,6,5:T(8,128)S(1)}, f32[1,1,8,8,8,1,1,128]{7,4,3,2,1,0,6,5:T(8,128)}, u32[]{:S(2)}) copy-start(f32[1,1,8,8,8,1,1,128]{7,4,3,2,1,0,6,5:T(8,128)} %copy-done.8) | copy-start | bytes 786436
  158.6 17.2 %copy-start.16 = (f32[8,8,8,1,1,128]{5,0,2,1,4,3:T(8,128)S(1)}, f32[8,8,8,1,1,128]{5,0,2,1,4,3:T(8,128)}, u32[]{:S(2)}) copy-start(f32[8,8,8,1,1,128]{5,0,2,1,4,3:T(8,128)} %copy-done.15) | copy-start | bytes 786436
  158.6 17.2 %copy-start.25 = (f32[1,1,8,8,8,1,1,128]{7,4,3,2,1,0,6,5:T(8,128)S(1)}, f32[1,1,8,8,8,1,1,128]{7,4,3,2,1,0,6,5:T(8,128)}, u32[]{:S(2)}) copy-start(f32[1,1,8,8,8,1,1,128]{7,4,3,2,1,0,6,5:T(8,128)} %copy-done.24) | copy-start | bytes 786436
  159.9 6.2 %collective-permute-start.3 = (f32[2,8,1,8,1,1,128]{6,1,3,2,5,4,0:T(8,128)S(1)}, f32[2,8,1,8,1,1,128]{6,1,3,2,5,4,0:T(8,128)S(1)}, u32[]{:S(2)}, u32[]{:S(2)}) collective-permute-start(f32[2,8,1,8,1,1,128]{6,1,3,2,5,4,0:T(8,128)S(1)} %get-tuple-element.70), channel_id=1, source_target_pairs={{1,0},{2,1},{3,2},{5,4},{6,5},{7,6},{9,8},{10,9},{11,10},{13,12},{... | collective-permute-start | bytes 196616 | tf_op jit(solution)/shard_map/ppermute | solution.py:16
  166.8 31.5 %copy-start.6 = (f32[2,8,8,8,1,1,128]{6,1,3,2,5,4,0:T(8,128)}, f32[2,8,8,8,1,1,128]{6,1,3,2,5,4,0:T(8,128)S(1)}, u32[]{:S(2)}) copy-start(f32[2,8,8,8,1,1,128]{6,1,3,2,5,4,0:T(8,128)S(1)} %get-tuple-element.59) | copy-start | bytes 1572868
  212.1 28.0 %all-to-all-start.2 = ((f32[32,1,128]{2,1,0:T(1,128)}), f32[32,1,128]{2,1,0:T(1,128)S(1)}, u32[]{:S(2)}, u32[]{:S(2)}) async-start(f32[32,1,128]{2,1,0:T(1,128)} %bitcast.160), calls=%async_computation.2 | async-start | bytes 32768 | tf_op jit(solution)/shard_map/all_to_all | solution.py:154
  273.3 23.1 %copy-start.5 = (f32[8,8,1,1]{1,0,3,2:T(8,128)S(1)}, f32[8,8,1,1]{1,0,3,2:T(8,128)}, u32[]{:S(2)}) copy-start(f32[8,8,1,1]{1,0,3,2:T(8,128)} %constant.406) | copy-start | bytes 772
  273.3 25.6 %copy-start.23 = (f32[8,8,8]{0,2,1:T(8,128)S(1)}, f32[8,8,8]{0,2,1:T(8,128)}, u32[]{:S(2)}) copy-start(f32[8,8,8]{0,2,1:T(8,128)} %copy-done.20) | copy-start | bytes 6148
  273.4 25.6 %copy-start.51 = (f32[128]{0:T(128)S(1)}, f32[128]{0:T(128)}, u32[]{:S(2)}) copy-start(f32[128]{0:T(128)} %copy-done.49) | copy-start | bytes 1540
  273.4 25.6 %copy-start.55 = (f32[128]{0:T(128)S(1)}, f32[128]{0:T(128)}, u32[]{:S(2)}) copy-start(f32[128]{0:T(128)} %copy-done.52) | copy-start | bytes 1540
  273.4 5.6 %collective-permute-start.9 = (f32[2,1,8,8,1,1,128]{6,1,3,2,5,4,0:T(1,128)S(1)}, f32[2,1,8,8,1,1,128]{6,1,3,2,5,4,0:T(1,128)S(1)}, u32[]{:S(2)}, u32[]{:S(2)}) collective-permute-start(f32[2,1,8,8,1,1,128]{6,1,3,2,5,4,0:T(1,128)S(1)} %bitcast.614), channel_id=1, source_target_pairs={{4,0},{8,4},{12,8},{16,12},{20,16},{24,20},{28,24},{5,1},{9,5},{13... | collective-permute-start | bytes 196616 | tf_op jit(solution)/shard_map/ppermute | solution.py:16
  276.1 5.9 %collective-permute-start.8 = (f32[2,1,8,8,1,1,128]{6,1,3,2,5,4,0:T(1,128)S(1)}, f32[2,1,8,8,1,1,128]{6,1,3,2,5,4,0:T(1,128)S(1)}, u32[]{:S(2)}, u32[]{:S(2)}) collective-permute-start(f32[2,1,8,8,1,1,128]{6,1,3,2,5,4,0:T(1,128)S(1)} %bitcast.618), channel_id=1, source_target_pairs={{0,4},{4,8},{8,12},{12,16},{16,20},{20,24},{24,28},{1,5},{5,9},{9,... | collective-permute-start | bytes 196616 | tf_op jit(solution)/shard_map/ppermute | solution.py:16
  278.7 25.1 %copy-start.10 = (f32[1,1,8,8,8,1,1,128]{7,4,3,2,1,0,6,5:T(8,128)S(1)}, f32[1,1,8,8,8,1,1,128]{7,4,3,2,1,0,6,5:T(8,128)}, u32[]{:S(2)}) copy-start(f32[1,1,8,8,8,1,1,128]{7,4,3,2,1,0,6,5:T(8,128)} %copy-done.8) | copy-start | bytes 786436
  278.7 25.1 %copy-start.17 = (f32[8,8,8,1,1,128]{5,0,2,1,4,3:T(8,128)S(1)}, f32[8,8,8,1,1,128]{5,0,2,1,4,3:T(8,128)}, u32[]{:S(2)}) copy-start(f32[8,8,8,1,1,128]{5,0,2,1,4,3:T(8,128)} %copy-done.15) | copy-start | bytes 786436
  282.1 6.1 %collective-permute-start.10 = (f32[2,8,1,8,1,1,128]{6,1,3,2,5,4,0:T(8,128)S(1)}, f32[2,8,1,8,1,1,128]{6,1,3,2,5,4,0:T(8,128)S(1)}, u32[]{:S(2)}, u32[]{:S(2)}) collective-permute-start(f32[2,8,1,8,1,1,128]{6,1,3,2,5,4,0:T(8,128)S(1)} %pad_maximum_fusion.6), channel_id=1, source_target_pairs={{0,1},{1,2},{2,3},{4,5},{5,6},{6,7},{8,9},{9,10},{10,11},{12,13},{... | collective-permute-start | bytes 196616 | tf_op jit(solution)/shard_map/ppermute | solution.py:16
  288.3 6.2 %collective-permute-start.11 = (f32[2,8,1,8,1,1,128]{6,1,3,2,5,4,0:T(8,128)S(1)}, f32[2,8,1,8,1,1,128]{6,1,3,2,5,4,0:T(8,128)S(1)}, u32[]{:S(2)}, u32[]{:S(2)}) collective-permute-start(f32[2,8,1,8,1,1,128]{6,1,3,2,5,4,0:T(8,128)S(1)} %get-tuple-element.57), channel_id=1, source_target_pairs={{1,0},{2,1},{3,2},{5,4},{6,5},{7,6},{9,8},{10,9},{11,10},{13,12},{... | collective-permute-start | bytes 196616 | tf_op jit(solution)/shard_map/ppermute | solution.py:16
  341.7 22.9 %all-to-all-start.3 = ((f32[32,1,128]{2,1,0:T(1,128)}), f32[32,1,128]{2,1,0:T(1,128)S(1)}, u32[]{:S(2)}, u32[]{:S(2)}) async-start(f32[32,1,128]{2,1,0:T(1,128)} %bitcast.209), calls=%async_computation.3 | async-start | bytes 32768 | tf_op jit(solution)/shard_map/all_to_all | solution.py:154
  352.5 24.0 %copy-start.46 = (f32[2048]{0:T(1024)S(1)}, f32[2048]{0:T(1024)}, u32[]{:S(2)}) copy-start(f32[2048]{0:T(1024)} %copy-done.45) | copy-start | bytes 24580
  352.5 24.0 %copy-start.44 = (s32[2048]{0:T(1024)S(1)}, s32[2048]{0:T(1024)}, u32[]{:S(2)}) copy-start(s32[2048]{0:T(1024)} %copy-done.43) | copy-start | bytes 24580
  388.5 23.1 %copy-start.2 = (f32[2,8,8,8,1,1,128]{6,3,2,1,0,5,4:T(8,128)S(1)}, f32[2,8,8,8,1,1,128]{6,3,2,1,0,5,4:T(8,128)}, u32[]{:S(2)}) copy-start(f32[2,8,8,8,1,1,128]{6,3,2,1,0,5,4:T(8,128)} %copy-done.1) | copy-start | bytes 1572868
  388.5 5.7 %collective-permute-start.13 = (f32[2,1,8,8,1,1,128]{6,1,3,2,5,4,0:T(1,128)S(1)}, f32[2,1,8,8,1,1,128]{6,1,3,2,5,4,0:T(1,128)S(1)}, u32[]{:S(2)}, u32[]{:S(2)}) collective-permute-start(f32[2,1,8,8,1,1,128]{6,1,3,2,5,4,0:T(1,128)S(1)} %bitcast.616), channel_id=1, source_target_pairs={{4,0},{8,4},{12,8},{16,12},{20,16},{24,20},{28,24},{5,1},{9,5},{13... | collective-permute-start | bytes 196616 | tf_op jit(solution)/shard_map/ppermute | solution.py:16
  391.8 5.9 %collective-permute-start.12 = (f32[2,1,8,8,1,1,128]{6,1,3,2,5,4,0:T(1,128)S(1)}, f32[2,1,8,8,1,1,128]{6,1,3,2,5,4,0:T(1,128)S(1)}, u32[]{:S(2)}, u32[]{:S(2)}) collective-permute-start(f32[2,1,8,8,1,1,128]{6,1,3,2,5,4,0:T(1,128)S(1)} %bitcast.620), channel_id=1, source_target_pairs={{0,4},{4,8},{8,12},{12,16},{16,20},{20,24},{24,28},{1,5},{5,9},{9,... | collective-permute-start | bytes 196616 | tf_op jit(solution)/shard_map/ppermute | solution.py:16
  397.8 6.1 %collective-permute-start.14 = (f32[2,8,1,8,1,1,128]{6,1,3,2,5,4,0:T(8,128)S(1)}, f32[2,8,1,8,1,1,128]{6,1,3,2,5,4,0:T(8,128)S(1)}, u32[]{:S(2)}, u32[]{:S(2)}) collective-permute-start(f32[2,8,1,8,1,1,128]{6,1,3,2,5,4,0:T(8,128)S(1)} %pad_maximum_fusion.4), channel_id=1, source_target_pairs={{0,1},{1,2},{2,3},{4,5},{5,6},{6,7},{8,9},{9,10},{10,11},{12,13},{... | collective-permute-start | bytes 196616 | tf_op jit(solution)/shard_map/ppermute | solution.py:16
  403.9 6.2 %collective-permute-start.15 = (f32[2,8,1,8,1,1,128]{6,1,3,2,5,4,0:T(8,128)S(1)}, f32[2,8,1,8,1,1,128]{6,1,3,2,5,4,0:T(8,128)S(1)}, u32[]{:S(2)}, u32[]{:S(2)}) collective-permute-start(f32[2,8,1,8,1,1,128]{6,1,3,2,5,4,0:T(8,128)S(1)} %get-tuple-element.46), channel_id=1, source_target_pairs={{1,0},{2,1},{3,2},{5,4},{6,5},{7,6},{9,8},{10,9},{11,10},{13,12},{... | collective-permute-start | bytes 196616 | tf_op jit(solution)/shard_map/ppermute | solution.py:16
  (32 other events, 268.6 us)
where the time goes:
time: 418 us; the launch traced here: 413 us
  local copies, waits for them, and re-layouts  201 us (48%)
  other arithmetic  85.1 us (20%)
  starting transfers between devices  65 us (16%)
  matrix products  31.2 us (7%)
  waiting for transfers between devices  28.5 us (7%)
    gather x6, local copies, waits for them, and re-layouts, one_block(): element_values = element_rows[ids].reshape(-1, 8, 8, 8)  79.6 us
    ppermute x16, starting transfers between devices, passed_along(): lax.ppermute(value, axis, [(source, source + steps) for source in range(l...  47 us
    gather x3, local copies, waits for them, and re-layouts, rate(): current = values.reshape(-1)[flat_index]  44.4 us
    gather x3, local copies, waits for them, and re-layouts, rate(): donor_values = replies[target]  44.3 us
    scatter-add x3, other arithmetic, rate(): local = local.reshape(-1).at[flat_index].add(added).reshape(shape_full)  35.6 us
    ppermute x16, waiting for transfers between devices, passed_along(): lax.ppermute(value, axis, [(source, source + steps) for source in range(l...  26.1 us
    dot_general x6, other arithmetic, one_block(): jnp.einsum('nijk,ni,nj,nk->n', element_values, wx, wy, wz, precision=lax....  14.5 us
    gather x1, local copies, waits for them, and re-layouts, body(): point_mass = volume_factor * cube_flat[point_q]  13.2 us
  transfers between devices with their start and end apart: 20, of which 10 were waited for; matrix products, arithmetic and copies ran while one was open for 39% of the time, Pallas kernels for 0%

commit v1 on v0

v1 whole, which is shorter than its diff:
```python
import functools
import jax
import jax.numpy as jnp
import numpy as np
from jax import lax
from jax.experimental import pallas as pl
from jax.experimental.pallas import tpu as pltpu
from jax.sharding import PartitionSpec as P

time_step = 0.01
penalty_rate = 50.0
metric = 2.0
volume_factor = 0.125
node_inner = [0.8717401485096066, 0.5917001814331423, 0.20929921790247888]


def legendre_seven(point):
    before, current = (1.0, point)
    for order in range(1, 7):
        before, current = (
            current,
            ((2 * order + 1) * point * current - order * before) / (order + 1),
        )
    return current


def gll_tables():
    degree = 7
    gll_nodes = [
        -1.0,
        -node_inner[0],
        -node_inner[1],
        -node_inner[2],
        node_inner[2],
        node_inner[1],
        node_inner[0],
        1.0,
    ]
    end_values = [legendre_seven(v) for v in gll_nodes]
    weights = [2.0 / (degree * (degree + 1) * v * v) for v in end_values]
    derivative = [[0.0] * 8 for _ in range(8)]
    for a in range(8):
        for b in range(8):
            if a != b:
                derivative[a][b] = end_values[a] / (end_values[b] * (gll_nodes[a] - gll_nodes[b]))
    derivative[0][0] = -degree * (degree + 1) / 4.0
    derivative[7][7] = degree * (degree + 1) / 4.0
    weight_row = jnp.asarray(weights, jnp.float32)
    cube_weights = weight_row[:, None, None] * weight_row[None, :, None] * weight_row[None, None, :]
    return (gll_nodes, cube_weights, derivative)


def lagrange_rows(position, gll_nodes):
    columns = []
    for j in range(8):
        factor = jnp.ones_like(position)
        for m in range(8):
            if m != j:
                factor = factor * ((position - gll_nodes[m]) / (gll_nodes[j] - gll_nodes[m]))
        columns.append(factor)
    return jnp.stack(columns, axis=-1)


MESH = pl.DeviceIdType.MESH
HEADINGS = [(-1, 0), (1, 0), (0, -1), (0, 1), (-1, -1), (-1, 1), (1, -1), (1, 1)]


def halves(value):
    high = value.astype(jnp.bfloat16)
    return high, (value - high.astype(jnp.float32)).astype(jnp.bfloat16)


def mm(a, b):
    return jnp.dot(a, b, preferred_element_type=jnp.float32)


def mm_t(a, b):
    return lax.dot_general(a, b, (((1,), (1,)), ((), ())), preferred_element_type=jnp.float32)


def mm3(op_high, op_low, value):
    high, low = halves(value)
    return mm(op_high, high) + mm(op_high, low) + mm(op_low, high)


def step_kernel(
    derivative, start_ref, vel_ref, nu_ref, wm_ref, dim_ref, ops_ref, basis_ref, donor_ref, slot_q_ref, slot_e_ref,
    out_ref,
    cur, local, work, grad, pick, spread_q, spread_e, count, ans, rep, hx, hy, he,
    ans_send, ans_recv, halo_send, halo_recv,
):
    gx, gy = lax.axis_index("gx"), lax.axis_index("gy")
    nx, ny = lax.axis_size("gx"), lax.axis_size("gy")
    n = nx * ny
    me = gx * ny + gy
    ez = start_ref.shape[-1]
    groups, _, lanes = donor_ref.shape
    cap = ans.shape[-1]
    per = lanes // cap

    barrier = pltpu.get_barrier_semaphore()

    def greet(step, carry):
        d = lax.rem(me + step, n)
        pl.semaphore_signal(barrier, inc=1, device_id=(d // ny, lax.rem(d, ny)), device_id_type=MESH)
        return carry

    hx[...] = jnp.zeros_like(hx)
    hy[...] = jnp.zeros_like(hy)
    he[...] = jnp.zeros_like(he)
    lax.fori_loop(1, n, greet, 0)

    count[...] = jnp.zeros_like(count)

    def build(g, carry):
        wide = lax.broadcasted_iota(jnp.int32, (2 * ez, lanes), 0)
        tall = lax.broadcasted_iota(jnp.int32, (512, lanes), 0)
        pick[g] = jnp.where(wide == donor_ref[g], 1.0, 0.0).astype(jnp.bfloat16)
        spread_e[g] = jnp.where(wide == slot_e_ref[g], 1.0, 0.0).astype(jnp.bfloat16)
        spread_q[g] = jnp.where(tall == slot_q_ref[g], 1.0, 0.0).astype(jnp.bfloat16)
        count[...] += mm_t(spread_q[g], spread_e[g])
        return carry

    lax.fori_loop(0, groups, build, 0)
    cur[...] = start_ref[...]
    pl.semaphore_wait(barrier, n - 1)

    def halo_copy(s, number):
        dx, dy = HEADINGS[number]
        rows = pl.ds(0 if dy < 0 else 56, 8)
        plane = 0 if dx < 0 else 7
        if dy == 0:
            source, target = local.at[:, plane], hx.at[s, number]
        elif dx == 0:
            source, target = local.at[:, :, rows, :], hy.at[s, number - 2]
        else:
            source, target = local.at[:, plane, rows, :], he.at[s, number - 4]
        return pltpu.make_async_remote_copy(
            src_ref=source, dst_ref=target, send_sem=halo_send.at[s, number], recv_sem=halo_recv.at[s, number],
            device_id=(gx + dx, gy + dy), device_id_type=MESH,
        )

    def inside(dx, dy):
        return (gx + dx >= 0) & (gx + dx < nx) & (gy + dy >= 0) & (gy + dy < ny)

    for s in range(3):
        both = jnp.concatenate([cur[0].reshape(512, ez), cur[1].reshape(512, ez)], axis=1)
        high, low = halves(both)

        def interpolate(g, carry):
            found = mm(high, pick[g]) + mm(low, pick[g])
            acc = found[0:64] * basis_ref[g, 0:1, :]
            for i in range(1, 8):
                acc = acc + found[64 * i:64 * i + 64] * basis_ref[g, i:i + 1, :]
            acc2 = acc[0:8] * basis_ref[g, 8:9, :]
            for j in range(1, 8):
                acc2 = acc2 + acc[8 * j:8 * j + 8] * basis_ref[g, 8 + j:9 + j, :]
            row = jnp.sum(acc2 * basis_ref[g, 16:24, :], axis=0, keepdims=True)
            for t in range(per):
                ans[s, g * per + t] = row[:, t * cap:(t + 1) * cap]
            return carry

        lax.fori_loop(0, groups, interpolate, 0)

        def send(step, carry):
            d = lax.rem(me + step, n)
            pltpu.make_async_remote_copy(
                src_ref=ans.at[s, d], dst_ref=rep.at[s, me], send_sem=ans_send.at[s], recv_sem=ans_recv.at[s],
                device_id=(d // ny, lax.rem(d, ny)), device_id_type=MESH,
            ).start()
            return carry

        lax.fori_loop(1, n, send, 0)

        for m in range(2):
            lo_lane = m * ez
            scale = nu_ref[m:m + 1, :]
            for half in range(2):
                part = cur[m, 4 * half:4 * half + 4].reshape(256, ez)
                grad[0, 4 * half:4 * half + 4, :, lo_lane:lo_lane + ez] = mm3(ops_ref[0], ops_ref[1], part).reshape(4, 64, ez)
                grad[1, 4 * half:4 * half + 4, :, lo_lane:lo_lane + ez] = mm3(ops_ref[2], ops_ref[3], part).reshape(4, 64, ez)
            for a in range(8):
                gxa = (2.0 * derivative[a][0]) * cur[m, 0]
                for i in range(1, 8):
                    gxa = gxa + (2.0 * derivative[a][i]) * cur[m, i]
                wm = wm_ref[a]
                gya = grad[0, a, :, lo_lane:lo_lane + ez]
                gza = grad[1, a, :, lo_lane:lo_lane + ez]
                adv = vel_ref[0, m, a] * gxa + vel_ref[1, m, a] * gya + vel_ref[2, m, a] * gza
                local[m, a] = -(wm * adv)
                wn = wm * scale
                work[m, a] = wn * gxa
                grad[0, a, :, lo_lane:lo_lane + ez] = wn * gya
                grad[1, a, :, lo_lane:lo_lane + ez] = wn * gza
            for half in range(2):
                part_y = grad[0, 4 * half:4 * half + 4, :, lo_lane:lo_lane + ez].reshape(256, ez)
                part_z = grad[1, 4 * half:4 * half + 4, :, lo_lane:lo_lane + ez].reshape(256, ez)
                back = mm3(ops_ref[4], ops_ref[5], part_y) + mm3(ops_ref[6], ops_ref[7], part_z)
                local[m, 4 * half:4 * half + 4] -= back.reshape(4, 64, ez)
            for i in range(8):
                total = (2.0 * derivative[0][i]) * work[m, 0]
                for a in range(1, 8):
                    total = total + (2.0 * derivative[a][i]) * work[m, a]
                local[m, i] -= total

        rep[s, me] = ans[s, me]
        whole = rep.at[s, pl.ds(0, n - 1)]
        pltpu.make_async_copy(whole, whole, ans_recv.at[s]).wait()

        work[...] = jnp.zeros_like(work)

        def scatter(g, carry):
            row = jnp.concatenate([rep[s, g * per + t] for t in range(per)], axis=1)
            row_high, row_low = halves(row)
            where_e = spread_e[g]
            added = mm_t(spread_q[g], where_e * row_high) + mm_t(spread_q[g], where_e * row_low)
            work[0] += added[:, :ez].reshape(8, 64, ez)
            work[1] += added[:, ez:].reshape(8, 64, ez)
            return carry

        lax.fori_loop(0, groups, scatter, 0)
        for m in range(2):
            for i in range(8):
                held = count[64 * i:64 * i + 64, m * ez:(m + 1) * ez]
                local[m, i] += penalty_rate * wm_ref[i] * (work[m, i] - held * cur[m, i])

        for number, (dx, dy) in enumerate(HEADINGS):
            @pl.when(inside(dx, dy))
            def _(number=number):
                halo_copy(s, number).start()

        for number, (dx, dy) in enumerate(HEADINGS):
            @pl.when(inside(-dx, -dy))
            def _(number=number):
                halo_copy(s, number).wait_recv()

        work[...] = local[...]
        for m in range(2):
            work[m, 7] += hx[s, 0, m]
            work[m, 0] += hx[s, 1, m]
            work[m, :, 56:64, :] += hy[s, 0, m]
            work[m, :, 0:8, :] += hy[s, 1, m]
            work[m, 7, 56:64, :] += he[s, 0, m]
            work[m, 7, 0:8, :] += he[s, 1, m]
            work[m, 0, 56:64, :] += he[s, 2, m]
            work[m, 0, 0:8, :] += he[s, 3, m]

        for m in range(2):
            flat = work[m].reshape(512, ez)
            depth = lax.rem(lax.broadcasted_iota(jnp.int32, (512, ez), 0), 8)
            lane = lax.broadcasted_iota(jnp.int32, (512, ez), 1)
            after = pltpu.roll(pltpu.roll(flat, 7, 0), ez - 1, 1)
            before = pltpu.roll(pltpu.roll(flat, 505, 0), 1, 1)
            flat = flat + jnp.where((depth == 7) & (lane < ez - 1), after, 0.0)
            flat = flat + jnp.where((depth == 0) & (lane > 0), before, 0.0)
            moved = cur[m] + flat.reshape(8, 64, ez) * dim_ref[...]
            if s == 0:
                cur[m] = moved
            elif s == 1:
                cur[m] = 0.75 * start_ref[m] + 0.25 * moved
            else:
                out_ref[m] = start_ref[m] / 3.0 + 2.0 / 3.0 * moved

        for number, (dx, dy) in enumerate(HEADINGS):
            @pl.when(inside(dx, dy))
            def _(number=number):
                halo_copy(s, number).wait_send()

    for s in range(3):
        whole = ans.at[s, pl.ds(0, n - 1)]
        pltpu.make_async_copy(whole, whole, ans_send.at[s]).wait()


def split_host(matrix):
    high = matrix.astype(jnp.bfloat16)
    low = (matrix - high.astype(np.float64)).astype(jnp.bfloat16)
    return [high, low]


def body(scalar, velocity, diffusivity, recv_owner, donor_elem, recv_point, recv_coords):
    gll_nodes, cube_weights, derivative = gll_tables()
    ez = scalar.shape[4]
    elems = scalar.shape[2] * scalar.shape[3] * ez
    width_x, width_y = lax.axis_size("gx"), lax.axis_size("gy")
    n = width_x * width_y
    rows = recv_owner.shape[0]
    cap = max(2, 2 * rows // n)
    slots_all = n * cap
    per = max(1, min(n, 512 // cap))
    groups, lanes = n // per, per * cap

    owners = recv_owner[:, 0]
    bf, f32 = jnp.bfloat16, jnp.float32
    hot = (owners[None, :] == jnp.arange(n, dtype=jnp.int32)[:, None]).astype(bf)
    width = min(256, rows)
    blocks = rows // width
    earlier = jnp.asarray(np.triu(np.ones((width, width)), 1), bf)
    hot3 = hot.reshape(n, blocks, width)
    within = jnp.einsum("nbr,rs->nbs", hot3, earlier, preferred_element_type=f32)
    sums = jnp.sum(hot3.astype(f32), axis=2)
    strict = np.triu(np.ones((blocks, blocks)), 1).astype(np.float32)
    offset = jnp.sum(sums[:, :, None] * strict[None], axis=1)
    rank = jnp.sum((within + offset[:, :, None]) * hot3.astype(f32), axis=0).reshape(rows)
    slot_hot = (rank[None, :].astype(jnp.int32) == jnp.arange(cap, dtype=jnp.int32)[:, None]).astype(bf)

    own_mesh = (jnp.arange(rows, dtype=jnp.int32) >= rows // 2).astype(jnp.int32)
    point_q, point_e = recv_point // elems, recv_point % elems
    high = lax.reduce_precision(recv_coords, 8, 7)
    middle = lax.reduce_precision(recv_coords - high, 8, 7)
    low = recv_coords - high - middle
    ints = jnp.stack([donor_elem, 1 - own_mesh, point_q // 8 + 1, point_q % 8, point_e, own_mesh]).astype(f32)
    data = jnp.concatenate([high, middle, low, ints], axis=0).astype(bf)
    routed = jnp.einsum("cnr,kr->nck", data[:, None, :] * hot[None], slot_hot, preferred_element_type=f32)
    coords = routed[:, 0:3] + routed[:, 3:6] + routed[:, 6:9]
    asked = jnp.concatenate([coords, routed[:, 9:10] + elems * routed[:, 10:11]], axis=1)
    received = lax.all_to_all(asked, ("gx", "gy"), split_axis=0, concat_axis=0, tiled=True)
    received = jnp.moveaxis(received.reshape(groups, per, 4, cap), 2, 1).reshape(groups, 4, lanes)

    def grouped(piece):
        return piece.astype(jnp.int32).reshape(groups, 1, lanes)

    slot_q = grouped((routed[:, 11] - 1.0) * 8.0 + routed[:, 12])
    slot_e = grouped(routed[:, 13] + elems * routed[:, 14])
    donor = received[:, 3:4].astype(jnp.int32)
    basis = jnp.moveaxis(lagrange_rows(received[:, 0:3], gll_nodes), 3, 2).reshape(groups, 24, lanes)

    half_eye = np.eye(4)
    table = 2.0 * np.asarray(derivative, np.float64)
    along_y = np.kron(half_eye, np.kron(table, np.eye(8)))
    along_z = np.kron(half_eye, np.kron(np.eye(8), table))
    ops = []
    for matrix in (along_y, along_z, along_y.T, along_z.T):
        ops = ops + split_host(matrix)
    ops = jnp.asarray(np.stack(ops))

    weights = np.asarray([2.0 / (56.0 * legendre_seven(v) ** 2) for v in gll_nodes], np.float64)
    shared = jnp.asarray(weights + weights[::-1] * (np.arange(8) % 7 == 0), f32)
    single = jnp.asarray(weights, f32)
    ends = jnp.arange(8)

    def line_mass(position, count):
        joined = ((ends == 0) & (position > 0)) | ((ends == 7) & (position < count - 1))
        return jnp.where(joined, shared, single)

    mass_x = line_mass(lax.axis_index("gx"), width_x)
    mass_y = line_mass(lax.axis_index("gy"), width_y)
    place = jnp.arange(ez)[None, :]
    joined_z = ((ends[:, None] == 0) & (place > 0)) | ((ends[:, None] == 7) & (place < ez - 1))
    mass_z = jnp.where(joined_z, shared[:, None], single[:, None])
    mass = volume_factor * mass_x[:, None, None, None] * mass_y[None, :, None, None] * mass_z[None, None]
    step_mass = (time_step / mass).reshape(8, 64, ez)
    wm = jnp.broadcast_to((volume_factor * cube_weights).reshape(8, 64, 1), (8, 64, ez))

    vmem = pltpu.VMEM
    out = pl.pallas_call(
        functools.partial(step_kernel, derivative),
        out_shape=jax.ShapeDtypeStruct((2, 8, 64, ez), f32),
        in_specs=[pl.BlockSpec(memory_space=vmem)] * 10,
        out_specs=pl.BlockSpec(memory_space=vmem),
        scratch_shapes=[
            vmem((2, 8, 64, ez), f32),
            vmem((2, 8, 64, ez), f32),
            vmem((2, 8, 64, ez), f32),
            vmem((2, 8, 64, 2 * ez), f32),
            vmem((groups, 2 * ez, lanes), bf),
            vmem((groups, 512, lanes), bf),
            vmem((groups, 2 * ez, lanes), bf),
            vmem((512, 2 * ez), f32),
            vmem((3, n, 1, cap), f32),
            vmem((3, n, 1, cap), f32),
            vmem((3, 2, 2, 64, ez), f32),
            vmem((3, 2, 2, 8, 8, ez), f32),
            vmem((3, 4, 2, 8, ez), f32),
            pltpu.SemaphoreType.DMA((3,)),
            pltpu.SemaphoreType.DMA((3,)),
            pltpu.SemaphoreType.DMA((3, 8)),
            pltpu.SemaphoreType.DMA((3, 8)),
        ],
        compiler_params=pltpu.CompilerParams(collective_id=0, has_side_effects=True),
        name="advance",
    )(
        scalar.reshape(2, 8, 64, ez), velocity.reshape(3, 2, 8, 64, ez), diffusivity.reshape(2, ez),
        wm, step_mass, ops, basis, donor, slot_q, slot_e,
    )
    return out.reshape(scalar.shape)


def solution(mesh):
    return jax.shard_map(
        body,
        mesh=mesh,
        in_specs=(
            P(None, None, "gx", "gy", None),
            P(None, None, None, "gx", "gy", None),
            P(None, "gx", "gy", None),
            P(("gx", "gy"), None),
            P(("gx", "gy")),
            P(("gx", "gy")),
            P(None, ("gx", "gy")),
        ),
        out_specs=P(None, None, "gx", "gy", None),
        check_vma=False,
    )
```

time: 418 us -> 87.7 us (0.21)
  local copies, waits for them, and re-layouts: 201 us -> 6.26 us
  other arithmetic: 85.1 us -> 7.79 us
  Pallas kernels: 0 us -> 60.2 us
  starting transfers between devices: 65 us -> 6.32 us
  matrix products: 31.2 us -> 1.81 us
  waiting for transfers between devices: 28.5 us -> 4.07 us
    gather x13 -> x0, local copies, waits for them, and re-layouts: 182 us -> none  [the longest x6 79.6 us: one_block(): element_values = element_rows[ids].reshape(-1, 8, 8, 8)]
    pallas_call x0 -> x1, Pallas kernels: none -> 60.2 us  [body(): pl.pallas_call(functools.partial(step_kernel, derivative), out_shape=jax....]
    ppermute x16 -> x0, starting transfers between devices: 47 us -> none  [passed_along(): lax.ppermute(value, axis, [(source, source + steps) for source in range(l...]
    scatter-add x3 -> x0, other arithmetic: 35.6 us -> none  [rate(): local = local.reshape(-1).at[flat_index].add(added).reshape(shape_full)]
    dot_general x36 -> x2, matrix products: 31.2 us -> 1.81 us  [the longest x1 1.12 us: body(): jnp.einsum('nbr,rs->nbs', hot3, earlier, preferred_element_type=f32)]
    ppermute x16 -> x0, waiting for transfers between devices: 26.1 us -> none  [passed_along(): lax.ppermute(value, axis, [(source, source + steps) for source in range(l...]
    dot_general x6 -> x0, other arithmetic: 14.5 us -> none  [one_block(): jnp.einsum('nijk,ni,nj,nk->n', element_values, wx, wy, wz, precision=lax....]
    all_to_all x4 -> x1, starting transfers between devices: 18 us -> 6.32 us  [body(): lax.all_to_all(asked, ('gx', 'gy'), split_axis=0, concat_axis=0, tiled=True)]
  transfers between devices with their start and end apart: 20 -> 1, of which waited for: 10 -> 1; matrix products, arithmetic and copies ran while one was open for 39% -> 2% of each run, Pallas kernels for 0% -> 0%
where the time goes in v1:
time: 87.7 us; the launch traced here: 86.6 us
  Pallas kernels  60.2 us (69%)
  other arithmetic  7.79 us (9%)
  starting transfers between devices  6.32 us (7%)
  local copies, waits for them, and re-layouts  6.26 us (7%)
  waiting for transfers between devices  4.07 us (5%)
  matrix products  1.81 us (2%)
    pallas_call x1, Pallas kernels, body(): pl.pallas_call(functools.partial(step_kernel, derivative), out_shape=jax....  60.2 us
    all_to_all x1, starting transfers between devices, body(): lax.all_to_all(asked, ('gx', 'gy'), split_axis=0, concat_axis=0, tiled=True)  6.32 us
    all_to_all x1, waiting for transfers between devices, body(): lax.all_to_all(asked, ('gx', 'gy'), split_axis=0, concat_axis=0, tiled=True)  4.07 us
    unnamed x7, local copies, waits for them, and re-layouts  2.4 us
    unnamed x9, other arithmetic  2.14 us
  transfers between devices with their start and end apart: 1, of which 1 were waited for; matrix products, arithmetic and copies ran while one was open for 2% of the time, Pallas kernels for 0%

profile of v1, /device:TPU:9, one launch (start us, length us, event | category | flops | bytes accessed | tf_op | source)
XLA Modules:
  0.0 86.6 jit_solution(17617734958096542094)
XLA Ops:
  0.0 0.7 add_select_fusion
  0.7 0.8 stack.48
  1.5 0.8 reduce-precision_convert_fusion.1
  2.3 0.5 broadcast.624
  2.8 1.4 %reduce.3 = s32[2048]{0:T(1024)S(1)} reduce(s32[2048,1]{0,1:T(1,128)} %param.16, s32[]{:T(128)} %broadcast.624), dimensions={1}, to_apply=%param.16.reduce_sub_computation.3 | reduce | bytes 16388 | tf_op args[3]
  4.2 0.1 convert_reduce_fusion
  4.3 0.1 copy.34
  4.4 0.8 multiply_reduce_fusion
  5.2 0.1 copy.35
  5.2 1.1 %fusion.6 = f32[8,256]{1,0:T(8,128)S(1)} fusion(bf16[256,256,1]{1,0,2:T(8,128)(2,1)} %constant.245, f32[32,8]{1,0:T(8,128)S(1)} %copy.35, s32[8,256]{1,0:T(8,128)S(1)} %eq.75), kind=kOutput, calls=%fused_computation.5 | convolution fusion | flops 34011136 | bytes 148480 | tf_op jit(solution)/shard_map/nbr,rs->nbs/dot_general | solution.py:299
  6.4 0.7 fusion.13
  7.1 0.1 pad_maximum_fusion
  7.2 0.0 copy-start
  7.2 0.0 copy-start.1
  7.2 0.7 fusion.3
  7.9 0.6 fusion.17
  8.6 0.7 copy.36
  9.2 6.3 %all-to-all-start = ((f32[32,4,128]{2,1,0:T(4,128)}), f32[32,4,128]{2,1,0:T(4,128)S(1)}, u32[]{:S(2)}, u32[]{:S(2)}) async-start(f32[32,4,128]{2,1,0:T(4,128)} %copy.36), calls=%async_computation | async-start | bytes 131072 | tf_op jit(solution)/shard_map/all_to_all | solution.py:316
  15.6 0.0 copy-done
  15.6 0.1 broadcast_multiply_fusion.1
  15.7 0.0 copy-done.1
  15.7 0.1 broadcast_multiply_fusion
  15.8 0.1 mul.314
  15.8 0.1 mul.315
  15.9 0.1 or_select_fusion
  16.0 0.1 mul.303
  16.1 0.1 mul.304
  16.2 0.1 mul.305
  16.2 0.9 multiply_divide_fusion.dim_ref
  17.1 4.1 %all-to-all-done = f32[32,4,128]{2,1,0:T(4,128)S(1)} async-done(((f32[32,4,128]{2,1,0:T(4,128)}), f32[32,4,128]{2,1,0:T(4,128)S(1)}, u32[]{:S(2)}, u32[]{:S(2)}) %all-to-all-start) | async-done | bytes 65568 | tf_op jit(solution)/shard_map/all_to_all | solution.py:316
  21.2 0.1 bitcast_dynamic-update-slice_fusion.7
  21.4 0.6 slice_convert_fusion.donor_ref
  22.0 0.1 bitcast_dynamic-update-slice_fusion.6
  22.1 0.1 bitcast_dynamic-update-slice_fusion.5
  22.2 0.1 bitcast_dynamic-update-slice_fusion.4
  22.3 0.1 bitcast_dynamic-update-slice_fusion.3
  22.4 0.1 bitcast_dynamic-update-slice_fusion.2
  22.5 0.1 bitcast_dynamic-update-slice_fusion.1
  22.6 0.1 bitcast_dynamic-update-slice_fusion
  22.8 1.0 %copy.44 = f32[8,3,8,512]{3,2,1,0:T(8,128)} copy(f32[8,3,8,512]{3,1,0,2:T(4,128)S(1)} %bitcast.53) | data formatting | bytes 786432 | tf_op jit(solution)/shard_map/transpose | solution.py:325
  23.7 0.8 broadcast_in_dim.12.wm_ref
  24.6 60.2 %advance.1 = f32[2,8,64,128]{3,2,1,0:T(8,128)} custom-call(f32[2,8,64,128]{3,2,1,0:T(8,128)} %bitcast.54, f32[3,2,8,64,128]{4,3,2,1,0:T(8,128)} %bitcast.51, f32[2,128]{1,0:T(2,128)} %bitcast.65, f32[8,64,128]{2,1,0:T(8,128)} %broadcast_in_dim.12.wm_ref, f32[8,64,128]{2,1,0:T(8,128)} %multiply_divide_fusion.dim_ref, ...), custom_call_target="tpu_custom_call" | custom-call | tf_op jit(solution)/shard_map/advance/pallas_call | solution.py:355
  84.8 1.9 %copy.54 = f32[2,512,1,1,128]{4,3,2,1,0:T(1,128)} copy(f32[2,512,1,1,128]{4,3,2,1,0:T(1,128)} %bitcast.50) | data formatting | bytes 1048576
  (16 shorter events, 0.1 us)
Async XLA Ops:
  7.2 8.4 %copy-start = (f32[8]{0:T(128)S(1)}, f32[8]{0:T(128)}, u32[]{:S(2)}) copy-start(f32[8]{0:T(128)} %constant.236.clone) | copy-start | bytes 100
  7.2 8.5 %copy-start.1 = (f32[8]{0:T(128)S(1)}, f32[8]{0:T(128)}, u32[]{:S(2)}) copy-start(f32[8]{0:T(128)} %constant.240.clone) | copy-start | bytes 100
  9.2 11.9 %all-to-all-start = ((f32[32,4,128]{2,1,0:T(4,128)}), f32[32,4,128]{2,1,0:T(4,128)S(1)}, u32[]{:S(2)}, u32[]{:S(2)}) async-start(f32[32,4,128]{2,1,0:T(4,128)} %copy.36), calls=%async_computation | async-start | bytes 131072 | tf_op jit(solution)/shard_map/all_to_all | solution.py:316

commit v2 on v1

--- a/solution.py
+++ b/solution.py
@@ -50,17 +50,6 @@
     return (gll_nodes, cube_weights, derivative)
 
 
-def lagrange_rows(position, gll_nodes):
-    columns = []
-    for j in range(8):
-        factor = jnp.ones_like(position)
-        for m in range(8):
-            if m != j:
-                factor = factor * ((position - gll_nodes[m]) / (gll_nodes[j] - gll_nodes[m]))
-        columns.append(factor)
-    return jnp.stack(columns, axis=-1)
-
-
 MESH = pl.DeviceIdType.MESH
 HEADINGS = [(-1, 0), (1, 0), (0, -1), (0, 1), (-1, -1), (-1, 1), (1, -1), (1, 1)]
 
@@ -84,9 +73,10 @@
 
 
 def step_kernel(
-    derivative, start_ref, vel_ref, nu_ref, wm_ref, dim_ref, ops_ref, basis_ref, donor_ref, slot_q_ref, slot_e_ref,
+    derivative, gll_nodes, start_ref, vel_ref, nu_ref, wm_ref, dim_ref, ops_ref, asked_ref, slot_q_ref, slot_e_ref,
     out_ref,
-    cur, local, work, grad, pick, spread_q, spread_e, count, ans, rep, hx, hy, he,
+    cur, local, work, grad, pick, spread_q, spread_e, count, ans, rep, hx, hy, he, got, basis_ref,
+    ask_send, ask_recv,
     ans_send, ans_recv, halo_send, halo_recv,
 ):
     gx, gy = lax.axis_index("gx"), lax.axis_index("gy")
@@ -94,7 +84,7 @@
     n = nx * ny
     me = gx * ny + gy
     ez = start_ref.shape[-1]
-    groups, _, lanes = donor_ref.shape
+    groups, _, lanes = slot_q_ref.shape
     cap = ans.shape[-1]
     per = lanes // cap
 
@@ -110,12 +100,22 @@
     he[...] = jnp.zeros_like(he)
     lax.fori_loop(1, n, greet, 0)
 
+    pl.semaphore_wait(barrier, n - 1)
+
+    def ask(step, carry):
+        d = lax.rem(me + step, n)
+        pltpu.make_async_remote_copy(
+            src_ref=asked_ref.at[d], dst_ref=got.at[me], send_sem=ask_send, recv_sem=ask_recv,
+            device_id=(d // ny, lax.rem(d, ny)), device_id_type=MESH,
+        ).start()
+        return carry
+
+    lax.fori_loop(1, n, ask, 0)
     count[...] = jnp.zeros_like(count)
 
     def build(g, carry):
         wide = lax.broadcasted_iota(jnp.int32, (2 * ez, lanes), 0)
         tall = lax.broadcasted_iota(jnp.int32, (512, lanes), 0)
-        pick[g] = jnp.where(wide == donor_ref[g], 1.0, 0.0).astype(jnp.bfloat16)
         spread_e[g] = jnp.where(wide == slot_e_ref[g], 1.0, 0.0).astype(jnp.bfloat16)
         spread_q[g] = jnp.where(tall == slot_q_ref[g], 1.0, 0.0).astype(jnp.bfloat16)
         count[...] += mm_t(spread_q[g], spread_e[g])
@@ -123,7 +123,24 @@
 
     lax.fori_loop(0, groups, build, 0)
     cur[...] = start_ref[...]
-    pl.semaphore_wait(barrier, n - 1)
+    got[me] = asked_ref[me]
+    first = got.at[pl.ds(0, n - 1)]
+    pltpu.make_async_copy(first, first, ask_recv).wait()
+
+    def prepare(g, carry):
+        asked = jnp.concatenate([got[g * per + t] for t in range(per)], axis=1)
+        wide = lax.broadcasted_iota(jnp.int32, (2 * ez, lanes), 0)
+        pick[g] = jnp.where(wide == asked[3:4].astype(jnp.int32), 1.0, 0.0).astype(jnp.bfloat16)
+        for j in range(8):
+            factor = jnp.ones_like(asked)
+            for k in range(8):
+                if k != j:
+                    factor = factor * ((asked - gll_nodes[k]) * (1.0 / (gll_nodes[j] - gll_nodes[k])))
+            for c in range(3):
+                basis_ref[g, 8 * c + j:8 * c + j + 1, :] = factor[c:c + 1]
+        return carry
+
+    lax.fori_loop(0, groups, prepare, 0)
 
     def halo_copy(s, number):
         dx, dy = HEADINGS[number]
@@ -259,13 +276,15 @@
             elif s == 1:
                 cur[m] = 0.75 * start_ref[m] + 0.25 * moved
             else:
-                out_ref[m] = start_ref[m] / 3.0 + 2.0 / 3.0 * moved
+                out_ref[m] = 2.0 / 3.0 * moved
 
         for number, (dx, dy) in enumerate(HEADINGS):
             @pl.when(inside(dx, dy))
             def _(number=number):
                 halo_copy(s, number).wait_send()
 
+    sent = got.at[pl.ds(0, n - 1)]
+    pltpu.make_async_copy(sent, sent, ask_send).wait()
     for s in range(3):
         whole = ans.at[s, pl.ds(0, n - 1)]
         pltpu.make_async_copy(whole, whole, ans_send.at[s]).wait()
@@ -313,17 +332,11 @@
     routed = jnp.einsum("cnr,kr->nck", data[:, None, :] * hot[None], slot_hot, preferred_element_type=f32)
     coords = routed[:, 0:3] + routed[:, 3:6] + routed[:, 6:9]
     asked = jnp.concatenate([coords, routed[:, 9:10] + elems * routed[:, 10:11]], axis=1)
-    received = lax.all_to_all(asked, ("gx", "gy"), split_axis=0, concat_axis=0, tiled=True)
-    received = jnp.moveaxis(received.reshape(groups, per, 4, cap), 2, 1).reshape(groups, 4, lanes)
-
     def grouped(piece):
         return piece.astype(jnp.int32).reshape(groups, 1, lanes)
 
     slot_q = grouped((routed[:, 11] - 1.0) * 8.0 + routed[:, 12])
     slot_e = grouped(routed[:, 13] + elems * routed[:, 14])
-    donor = received[:, 3:4].astype(jnp.int32)
-    basis = jnp.moveaxis(lagrange_rows(received[:, 0:3], gll_nodes), 3, 2).reshape(groups, 24, lanes)
-
     half_eye = np.eye(4)
     table = 2.0 * np.asarray(derivative, np.float64)
     along_y = np.kron(half_eye, np.kron(table, np.eye(8)))
@@ -353,9 +366,9 @@
 
     vmem = pltpu.VMEM
     out = pl.pallas_call(
-        functools.partial(step_kernel, derivative),
+        functools.partial(step_kernel, derivative, gll_nodes),
         out_shape=jax.ShapeDtypeStruct((2, 8, 64, ez), f32),
-        in_specs=[pl.BlockSpec(memory_space=vmem)] * 10,
+        in_specs=[pl.BlockSpec(memory_space=vmem)] * 9,
         out_specs=pl.BlockSpec(memory_space=vmem),
         scratch_shapes=[
             vmem((2, 8, 64, ez), f32),
@@ -371,6 +384,10 @@
             vmem((3, 2, 2, 64, ez), f32),
             vmem((3, 2, 2, 8, 8, ez), f32),
             vmem((3, 4, 2, 8, ez), f32),
+            vmem((n, 4, cap), f32),
+            vmem((groups, 24, lanes), f32),
+            pltpu.SemaphoreType.DMA,
+            pltpu.SemaphoreType.DMA,
             pltpu.SemaphoreType.DMA((3,)),
             pltpu.SemaphoreType.DMA((3,)),
             pltpu.SemaphoreType.DMA((3, 8)),
@@ -380,9 +397,9 @@
         name="advance",
     )(
         scalar.reshape(2, 8, 64, ez), velocity.reshape(3, 2, 8, 64, ez), diffusivity.reshape(2, ez),
-        wm, step_mass, ops, basis, donor, slot_q, slot_e,
+        wm, step_mass, ops, asked, slot_q, slot_e,
     )
-    return out.reshape(scalar.shape)
+    return scalar / 3.0 + out.reshape(scalar.shape)
 
 
 def solution(mesh):

time: 87.7 us -> 84.7 us (0.966)
  Pallas kernels: 60.2 us -> 66.8 us
  starting transfers between devices: 6.32 us -> 0 us
  waiting for transfers between devices: 4.07 us -> 0 us
  other arithmetic: 7.79 us -> 11.6 us
  local copies, waits for them, and re-layouts: 6.26 us -> 3.48 us
    pallas_call x1, Pallas kernels: 60.2 us -> 66.8 us  [body(): pl.pallas_call(functools.partial(step_kernel, derivative, gll_nodes), out...]
    all_to_all x1 -> x0, starting transfers between devices: 6.32 us -> none  [body(): lax.all_to_all(asked, ('gx', 'gy'), split_axis=0, concat_axis=0, tiled=True)]
    all_to_all x1 -> x0, waiting for transfers between devices: 4.07 us -> none  [body(): lax.all_to_all(asked, ('gx', 'gy'), split_axis=0, concat_axis=0, tiled=True)]
    add x0 -> x1, other arithmetic: none -> 2.56 us  [body(): return scalar / 3.0 + out.reshape(scalar.shape)]
    unnamed x7 -> x4, local copies, waits for them, and re-layouts: 2.4 us -> 0.52 us
    transpose x1 -> x0, local copies, waits for them, and re-layouts: 0.98 us -> none  [body(): jnp.moveaxis(lagrange_rows(received[:, 0:3], gll_nodes), 3, 2)]
    unnamed x9 -> x2, other arithmetic: 2.14 us -> 1.37 us
  transfers between devices with their start and end apart: 1 -> 0, of which waited for: 1 -> 0; matrix products, arithmetic and copies ran while one was open for 2% -> 0% of each run, Pallas kernels for 0% -> 0%
where the time goes in v2:
time: 84.7 us; the launch traced here: 83.9 us
  Pallas kernels  66.8 us (79%)
  other arithmetic  11.6 us (14%)
  local copies, waits for them, and re-layouts  3.48 us (4%)
  matrix products  1.82 us (2%)
    pallas_call x1, Pallas kernels, body(): pl.pallas_call(functools.partial(step_kernel, derivative, gll_nodes), out...  66.8 us
    add x1, other arithmetic, body(): return scalar / 3.0 + out.reshape(scalar.shape)  2.56 us

profile of v2, /device:TPU:9, one launch (start us, length us, event | category | flops | bytes accessed | tf_op | source)
XLA Modules:
  0.0 83.9 jit_solution(6107799063079017723)
XLA Ops:
  0.0 0.7 fusion.23
  0.7 0.7 or_select_fusion
  1.4 0.1 broadcast_multiply_fusion
  1.5 0.7 mul.157
  2.2 0.1 mul.161
  2.3 0.8 broadcast_multiply_fusion.1
  3.1 0.5 broadcast.280
  3.6 1.4 %reduce.3 = s32[2048]{0:T(1024)S(1)} reduce(s32[2048,1]{0,1:T(1,128)} %param.16, s32[]{:T(128)} %broadcast.280), dimensions={1}, to_apply=%param.16.reduce_sub_computation.3 | reduce | bytes 16388 | tf_op args[3]
  5.0 0.1 convert_reduce_fusion
  5.1 0.1 copy.19
  5.2 0.8 multiply_reduce_fusion
  5.9 0.1 copy.20
  6.0 1.1 %fusion.3 = f32[8,256]{1,0:T(8,128)S(1)} fusion(bf16[256,256,1]{1,0,2:T(8,128)(2,1)} %constant.105, f32[32,8]{1,0:T(8,128)S(1)} %copy.20, s32[8,256]{1,0:T(8,128)S(1)} %eq.75), kind=kOutput, calls=%fused_computation.4 | convolution fusion | flops 34011136 | bytes 148480 | tf_op jit(solution)/shard_map/nbr,rs->nbs/dot_general | solution.py:318
  7.2 0.7 add_select_fusion
  7.9 0.8 stack.21
  8.7 0.1 mul.159
  8.7 0.1 mul.160
  8.8 0.1 mul.170
  8.9 0.1 mul.171
  9.0 0.8 reduce-precision_convert_fusion.1
  9.8 0.1 pad_maximum_fusion
  9.8 0.7 fusion.10
  10.6 0.7 fusion
  11.3 0.1 copy.25
  11.4 0.7 fusion.17
  12.2 0.6 pad_maximum_fusion.1.asked_ref
  12.8 0.8 %multiply_divide_fusion.dim_ref = f32[8,64,128]{2,1,0:T(8,128)} fusion(f32[64,128]{1,0:T(8,128)S(1)} %broadcast_bitcast_fusion, f32[8,64]{1,0:T(8,128)S(1)} %mul.171), kind=kLoop, calls=%fused_computation.16 | loop fusion | flops 131072 | bytes 296960 | tf_op jit(solution)/shard_map/div | solution.py:364
  13.7 0.8 broadcast_in_dim.12.wm_ref
  14.5 0.0 copy-start
  14.5 66.8 %advance.1 = f32[2,8,64,128]{3,2,1,0:T(8,128)} custom-call(f32[2,8,64,128]{3,2,1,0:T(8,128)} %bitcast.27, f32[3,2,8,64,128]{4,3,2,1,0:T(8,128)} %bitcast.29, f32[2,128]{1,0:T(2,128)} %bitcast.40, f32[8,64,128]{2,1,0:T(8,128)} %broadcast_in_dim.12.wm_ref, f32[8,64,128]{2,1,0:T(8,128)} %multiply_divide_fusion.dim_ref, ...), custom_call_target="tpu_custom_call" | custom-call | tf_op jit(solution)/shard_map/advance/pallas_call | solution.py:368
  81.3 0.0 copy-done
  81.3 2.6 %multiply_add_fusion = f32[2,512,1,1,128]{4,3,2,1,0:T(1,128)} fusion(f32[2,512,1,1,128]{4,3,2,1,0:T(1,128)} %bitcast.28, f32[2,512,1,1,128]{4,3,2,1,0:T(1,128)S(1)} %copy-done), kind=kLoop, calls=%fused_computation.10 | loop fusion | flops 262144 | bytes 1572864 | tf_op jit(solution)/shard_map/add | solution.py:402
  (11 shorter events, 0.1 us)
Async XLA Ops:
  14.5 66.8 %copy-start = (f32[2,512,1,1,128]{4,3,2,1,0:T(1,128)S(1)}, f32[2,512,1,1,128]{4,3,2,1,0:T(1,128)}, u32[]{:S(2)}) copy-start(f32[2,512,1,1,128]{4,3,2,1,0:T(1,128)} %param.13) | copy-start | bytes 1572868
